TPU v7x, 32 devices: a whole 2x2x4 slice. The times are simulated.
32 devices in a mesh: section: 2 (over x), row: 4 (over y, core), col: 4 (over z).
Axes of the slice: x: 2, y: 2, z: 4, core: 2. Of those that a mesh axis runs over, the one named last changes fastest.
Arguments:
- inputs: bfloat16 [2, 1024, 2048], P(None, 'col', 'row'), may hold values from -6 to 6
- positions: int32 [2, 1024], P(None, 'col'), may hold values from 0 to 765, as said below
- cotangent: bfloat16 [2, 1024, 2048], P(None, 'col', 'row'), may hold values from -6 to 6
- norm_gains: float32 [2, 2, 2048], P('section'), may hold values from 0.5 to 1.5
- norm_biases: float32 [2, 2, 2048], P('section'), may hold values from -2 to 2
- qkv_weight: bfloat16 [2, 2048, 6144], P('section', 'col', 'row')
- qkv_bias: float32 [2, 6144], P('section', 'row'), may hold values from -3 to 3
- dense_weight: bfloat16 [2, 2048, 2048], P('section', 'row', 'col'), may hold values from -0.375 to 0.375
- dense_bias: float32 [2, 2048], P('section', 'row'), may hold values from -2 to 2
- fc1_weight: bfloat16 [2, 2048, 8192], P('section', 'col', 'row'), may hold values from -0.125 to 0.125
- fc1_bias: float32 [2, 8192], P('section', 'row'), may hold values from -3 to 3
- fc2_weight: bfloat16 [2, 8192, 2048], P('section', 'row', 'col'), may hold values from -0.0625 to 0.0625
- fc2_bias: float32 [2, 2048], P('section', 'row'), may hold values from -2 to 2
Outputs:
- section_outputs: bfloat16 [2, 2, 1024, 2048], P('section', None, 'col', 'row')
- input_grads: float32 [2, 2, 1024, 2048], P('section', None, 'col', 'row')
- qkv_weight_grad: float32 [2, 2048, 6144], P('section', 'col', 'row')
- qkv_bias_grad: float32 [2, 6144], P('section', 'row')
- dense_weight_grad: float32 [2, 2048, 2048], P('section', 'row', 'col')
- out_bias_grad: float32 [2, 2048], P('section', 'row')
- fc1_weight_grad: float32 [2, 2048, 8192], P('section', 'col', 'row')
- fc1_bias_grad: float32 [2, 8192], P('section', 'row')
- fc2_weight_grad: float32 [2, 8192, 2048], P('section', 'row', 'col')
- norm_gain_grad: float32 [2, 2, 2048], P('section')
- norm_bias_grad: float32 [2, 2, 2048], P('section')
Inputs may be any that keep to these rules, and one draw needn't show every extreme that they name: Each sequence of 256 tokens starts at position 0, and positions rise by 1 to 3 from one token to the next; the first sequence of the first micro-batch rises by 3 at every token.
All inputs are finite; a program needn't handle non-finite values.
Results may differ from a plain program's by a relative error of at most 0.012.
Values may be sent and summed in bfloat16 or wider, within the bound.
A program may use at most 256 MiB of HBM per device.

v0:
```python
from functools import partial
import math

import jax
import jax.numpy as jnp
from jax import lax
from jax.sharding import PartitionSpec as P

HEAD_DIM = 256
ROT = 64
LEN = 256


NORM_EPS = 1e-05


def shifted(value, axis, steps):
    count = lax.axis_size(axis)
    initial, last = (max(0, -steps), min(count, count - steps))
    return lax.ppermute(value, axis, [(source, source + steps) for source in range(initial, last)])


def layer_norm(field_rows, gain, shift):
    center = field_rows - jnp.mean(field_rows, axis=-1, keepdims=True)
    rstd_value = lax.rsqrt(jnp.mean(center * center, axis=-1, keepdims=True) + NORM_EPS)
    normed = center * rstd_value
    return (normed * gain + shift, normed, rstd_value)


def norm_back(grad_rows, normed, rstd_value, gain):
    scaled = grad_rows * gain
    return rstd_value * (
        scaled
        - jnp.mean(scaled, axis=-1, keepdims=True)
        - normed * jnp.mean(scaled * normed, axis=-1, keepdims=True)
    )


def rotary_tables(place_ids, rotary_dims):
    half_dims = rotary_dims // 2
    powers = jnp.arange(half_dims).astype(jnp.float32) * (2.0 / rotary_dims)
    inverse = jnp.exp(-math.log(10000.0) * powers)
    angles = place_ids.astype(jnp.float32)[:, None] * inverse[None, :]
    return (jnp.cos(angles), jnp.sin(angles))


def rotate_pairs(vectors, cosines, sines, rotary_dims, direction):
    half_dims = rotary_dims // 2
    lower = vectors[..., :half_dims]
    upper = vectors[..., half_dims:rotary_dims]
    cos_part = cosines[:, None, :]
    sin_part = direction * sines[:, None, :]
    return jnp.concatenate(
        [
            lower * cos_part - upper * sin_part,
            upper * cos_part + lower * sin_part,
            vectors[..., rotary_dims:],
        ],
        axis=-1,
    )


def gelu_parts(pre_act):
    cdf_value = 0.5 * (1.0 + lax.erf(pre_act * 0.5**0.5))
    density = jnp.exp(-0.5 * pre_act * pre_act) * (2.0 * math.pi) ** (-0.5)
    return (pre_act * cdf_value, cdf_value + pre_act * density)


def causal_scores(query_seq, key_seq):
    length = query_seq.shape[1]
    scores = jnp.einsum(
        "sqhd,skhd->shqk", query_seq, key_seq, preferred_element_type=jnp.float32
    ) * query_seq.shape[-1] ** (-0.5)
    allowed = jnp.arange(length)[:, None] >= jnp.arange(length)[None, :]
    return jnp.where(allowed, scores, -jnp.inf)


def fetch_weights(shards):
    wide_qkv, wide_fc1 = (
        lax.all_gather(shards[0], "col", axis=0, tiled=True),
        lax.all_gather(shards[1], "col", axis=0, tiled=True),
    )
    wide_dense, wide_fc2 = (
        lax.all_gather(shards[2], "col", axis=1, tiled=True),
        lax.all_gather(shards[3], "col", axis=1, tiled=True),
    )
    return (wide_qkv, wide_fc1, wide_dense, wide_fc2)


def forward_slot(section_entry, place_ids, weights, params):
    w_qkv, w_fc1, w_dense, w_fc2 = weights
    norm_gain, norm_shift, b_qkv, b_fc1, b_dense, b_fc2 = params
    wide_input = lax.all_gather(section_entry, "row", axis=1, tiled=True)
    field_rows = wide_input.astype(jnp.float32)
    first_low = layer_norm(field_rows, norm_gain[0], norm_shift[0])[0].astype(jnp.bfloat16)
    second_low = layer_norm(field_rows, norm_gain[1], norm_shift[1])[0].astype(jnp.bfloat16)
    rows_count = wide_input.shape[0]
    local_heads = w_qkv.shape[1] // (3 * HEAD_DIM)
    mixed = (jnp.dot(first_low, w_qkv, preferred_element_type=jnp.float32) + b_qkv).reshape(
        rows_count, local_heads, 3, HEAD_DIM
    )
    cosines, sines = rotary_tables(place_ids, ROT)
    query_rows = rotate_pairs(mixed[:, :, 0], cosines, sines, ROT, 1.0).astype(jnp.bfloat16)
    key_rows = rotate_pairs(mixed[:, :, 1], cosines, sines, ROT, 1.0).astype(jnp.bfloat16)
    values = mixed[:, :, 2].astype(jnp.bfloat16)
    seq_shape = (rows_count // LEN, LEN, local_heads, HEAD_DIM)
    scores = causal_scores(query_rows.reshape(seq_shape), key_rows.reshape(seq_shape))
    row_top = jnp.max(scores, axis=-1, keepdims=True)
    logsum = row_top + jnp.log(jnp.sum(jnp.exp(scores - row_top), axis=-1, keepdims=True))
    probs = jnp.exp(scores - logsum).astype(jnp.bfloat16)
    attended = jnp.einsum(
        "shqk,skhd->sqhd", probs, values.reshape(seq_shape), preferred_element_type=jnp.float32
    )
    attn_out = attended.reshape(rows_count, local_heads * HEAD_DIM).astype(jnp.bfloat16)
    pre_act = jnp.dot(second_low, w_fc1, preferred_element_type=jnp.float32) + b_fc1
    activation = gelu_parts(pre_act)[0].astype(jnp.bfloat16)
    partial_sum = jnp.dot(attn_out, w_dense, preferred_element_type=jnp.float32) + jnp.dot(
        activation, w_fc2, preferred_element_type=jnp.float32
    )
    summed = lax.psum_scatter(partial_sum, "row", scatter_dimension=1, tiled=True)
    layer_output = (section_entry.astype(jnp.float32) + summed + b_dense + b_fc2).astype(
        jnp.bfloat16
    )
    return (
        layer_output,
        (wide_input, query_rows, key_rows, values, attn_out, logsum, pre_act, activation),
    )


def backward_slot(grad_entry, saved_state, place_ids, weights, params):
    wide_input, query_rows, key_rows, values, attn_out, logsum, pre_act, activation = saved_state
    w_qkv, w_fc1, w_dense, w_fc2 = weights
    norm_gain, norm_shift, b_qkv, b_fc1, b_dense, b_fc2 = params
    wide_grad = lax.all_gather(grad_entry, "row", axis=1, tiled=True)
    field_rows = wide_input.astype(jnp.float32)
    first_norm, first_hat, first_rstd = layer_norm(field_rows, norm_gain[0], norm_shift[0])
    second_norm, second_hat, second_rstd = layer_norm(field_rows, norm_gain[1], norm_shift[1])
    first_low = first_norm.astype(jnp.bfloat16)
    second_low = second_norm.astype(jnp.bfloat16)
    d_attn = jnp.dot(wide_grad, w_dense.T, preferred_element_type=jnp.float32).astype(jnp.bfloat16)
    d_activ = jnp.dot(wide_grad, w_fc2.T, preferred_element_type=jnp.float32)
    d_pre = d_activ * gelu_parts(pre_act)[1]
    d_pre_low = d_pre.astype(jnp.bfloat16)
    g_fc2 = jnp.dot(activation.T, wide_grad, preferred_element_type=jnp.float32)
    g_dense = jnp.dot(attn_out.T, wide_grad, preferred_element_type=jnp.float32)
    g_fc1 = jnp.dot(second_low.T, d_pre_low, preferred_element_type=jnp.float32)
    rows_count = wide_input.shape[0]
    local_heads = query_rows.shape[1]
    seq_shape = (rows_count // LEN, LEN, local_heads, HEAD_DIM)
    head_shape = (rows_count, local_heads, HEAD_DIM)
    query_seq = query_rows.reshape(seq_shape)
    key_seq = key_rows.reshape(seq_shape)
    grad_seq = d_attn.reshape(seq_shape)
    probs = jnp.exp(causal_scores(query_seq, key_seq) - logsum)
    d_values = jnp.einsum(
        "shqk,sqhd->skhd", probs.astype(jnp.bfloat16), grad_seq, preferred_element_type=jnp.float32
    )
    d_probs = jnp.einsum(
        "sqhd,skhd->shqk", grad_seq, values.reshape(seq_shape), preferred_element_type=jnp.float32
    )
    row_dots = jnp.einsum(
        "sqhd,sqhd->shq", grad_seq, attn_out.reshape(seq_shape), preferred_element_type=jnp.float32
    )[..., None]
    d_scores = (probs * (d_probs - row_dots) * HEAD_DIM ** (-0.5)).astype(jnp.bfloat16)
    d_query = jnp.einsum(
        "shqk,skhd->sqhd", d_scores, key_seq, preferred_element_type=jnp.float32
    ).reshape(head_shape)
    d_keys = jnp.einsum(
        "shqk,sqhd->skhd", d_scores, query_seq, preferred_element_type=jnp.float32
    ).reshape(head_shape)
    cosines, sines = rotary_tables(place_ids, ROT)
    d_query = rotate_pairs(d_query, cosines, sines, ROT, -1.0)
    d_keys = rotate_pairs(d_keys, cosines, sines, ROT, -1.0)
    d_mixed = jnp.stack([d_query, d_keys, d_values.reshape(head_shape)], axis=2).reshape(
        rows_count, 3 * local_heads * HEAD_DIM
    )
    d_mixed_low = d_mixed.astype(jnp.bfloat16)
    g_qkv = jnp.dot(first_low.T, d_mixed_low, preferred_element_type=jnp.float32)
    back_first = jnp.dot(d_mixed_low, w_qkv.T, preferred_element_type=jnp.float32)
    back_second = jnp.dot(d_pre_low, w_fc1.T, preferred_element_type=jnp.float32)
    back_first, back_second = lax.psum((back_first, back_second), "row")
    d_field = norm_back(back_first, first_hat, first_rstd, norm_gain[0]) + norm_back(
        back_second, second_hat, second_rstd, norm_gain[1]
    )
    feature_width = grad_entry.shape[1]
    d_input = grad_entry.astype(jnp.float32) + lax.dynamic_slice_in_dim(
        d_field, lax.axis_index("row") * feature_width, feature_width, 1
    )
    gain_terms = jnp.stack(
        [jnp.sum(back_first * first_hat, axis=0), jnp.sum(back_second * second_hat, axis=0)]
    )
    shift_terms = jnp.stack([jnp.sum(back_first, axis=0), jnp.sum(back_second, axis=0)])
    small_terms = (
        gain_terms,
        shift_terms,
        jnp.sum(d_mixed, axis=0),
        jnp.sum(d_pre, axis=0),
        jnp.sum(grad_entry.astype(jnp.float32), axis=0),
    )
    return (d_input, (g_qkv, g_fc1, g_dense, g_fc2), small_terms)


def reduce_grads(weight_terms, small_terms):
    part_qkv, part_fc1 = (
        lax.psum_scatter(weight_terms[0], "col", scatter_dimension=0, tiled=True),
        lax.psum_scatter(weight_terms[1], "col", scatter_dimension=0, tiled=True),
    )
    part_dense, part_fc2 = (
        lax.psum_scatter(weight_terms[2], "col", scatter_dimension=1, tiled=True),
        lax.psum_scatter(weight_terms[3], "col", scatter_dimension=1, tiled=True),
    )
    summed_small = lax.psum(
        (small_terms[0], small_terms[1], small_terms[2], small_terms[3], small_terms[4]), "col"
    )
    return ((part_qkv, part_fc1, part_dense, part_fc2), tuple(summed_small))


def add_terms(running, update):
    if running is None:
        return update
    return tuple((jnp.add(older, newer) for older, newer in zip(running, update)))


def local(
    inputs,
    positions,
    cotangent,
    norm_gains,
    norm_biases,
    qkv_weight,
    qkv_bias,
    dense_weight,
    dense_bias,
    fc1_weight,
    fc1_bias,
    fc2_weight,
    fc2_bias,
):
    micro_count = inputs.shape[0]
    first_section = lax.axis_index("section") == 0
    params = (norm_gains[0], norm_biases[0], qkv_bias[0], fc1_bias[0], dense_bias[0], fc2_bias[0])
    shards = (qkv_weight[0], fc1_weight[0], dense_weight[0], fc2_weight[0])
    received = jnp.zeros_like(inputs[0])
    results = []
    stores = []
    for tick_index in range(micro_count + 1):
        own_index = min(tick_index, micro_count - 1)
        prior_index = max(tick_index - 1, 0)
        section_entry = jnp.where(first_section, inputs[own_index], received)
        place_ids = jnp.where(first_section, positions[own_index], positions[prior_index])
        weights = fetch_weights(shards)
        result, saved_state = forward_slot(section_entry, place_ids, weights, params)
        results.append(result)
        stores.append(saved_state)
        if tick_index < micro_count:
            received = shifted(result, "section", 1)
    back_received = jnp.zeros_like(cotangent[0])
    input_terms = []
    weight_total = None
    small_total = None
    for tick_index in range(micro_count + 1):
        own_index = min(tick_index, micro_count - 1)
        prior_index = max(tick_index - 1, 0)
        later_index = min(tick_index + 1, micro_count)
        grad_entry = jnp.where(first_section, back_received, cotangent[own_index])
        place_ids = jnp.where(first_section, positions[prior_index], positions[own_index])
        saved_state = jax.tree.map(
            partial(jnp.where, first_section), stores[prior_index], stores[later_index]
        )
        active = jnp.where(
            first_section, float(tick_index >= 1), float(tick_index < micro_count)
        ).astype(jnp.float32)
        weights = fetch_weights(shards)
        d_input, weight_terms, small_terms = backward_slot(
            grad_entry, saved_state, place_ids, weights, params
        )
        input_terms.append(d_input)
        if tick_index < micro_count:
            back_received = shifted(d_input.astype(jnp.bfloat16), "section", -1)
        weight_terms = tuple((member * active for member in weight_terms))
        small_terms = tuple((member * active for member in small_terms))
        weight_total = add_terms(weight_total, weight_terms)
        small_total = add_terms(small_total, small_terms)
    weight_total, small_total = reduce_grads(weight_total, small_total)
    section_outputs = jnp.stack(
        [
            jnp.where(first_section, results[micro_index], results[micro_index + 1])
            for micro_index in range(micro_count)
        ]
    )[None]
    input_grads = jnp.stack(
        [
            jnp.where(first_section, input_terms[micro_index + 1], input_terms[micro_index])
            for micro_index in range(micro_count)
        ]
    )[None]
    return (
        section_outputs,
        input_grads,
        weight_total[0][None],
        small_total[2][None],
        weight_total[2][None],
        small_total[4][None],
        weight_total[1][None],
        small_total[3][None],
        weight_total[3][None],
        small_total[0][None],
        small_total[1][None],
    )


def solution(mesh):
    in_specs = (
        P(None, "col", "row"),
        P(None, "col"),
        P(None, "col", "row"),
        P("section", None, None),
        P("section", None, None),
        P("section", "col", "row"),
        P("section", "row"),
        P("section", "row", "col"),
        P("section", "row"),
        P("section", "col", "row"),
        P("section", "row"),
        P("section", "row", "col"),
        P("section", "row"),
    )
    out_specs = (
        P("section", None, "col", "row"),
        P("section", None, "col", "row"),
        P("section", "col", "row"),
        P("section", "row"),
        P("section", "row", "col"),
        P("section", "row"),
        P("section", "col", "row"),
        P("section", "row"),
        P("section", "row", "col"),
        P("section", None, None),
        P("section", None, None),
    )
    return jax.shard_map(local, mesh=mesh, in_specs=in_specs, out_specs=out_specs, check_vma=False)
```

profile of v0, /device:TPU:0, one launch (start us, length us, event | category | flops | bytes accessed | tf_op | source)
XLA Modules:
  0.0 1931.8 jit_solution(7486820466169379333)
XLA Ops:
  15.1 14.5 all-gather.25.cloned.1.call-done
  32.8 113.7 %all-gather.27.cloned.1.call-done = bf16[1,2048,1536]{2,1,0:T(8,128)(2,1)} async-done(((bf16[1,512,1536]{2,1,0:T(8,128)(2,1)}), bf16[1,2048,1536]{2,1,0:T(8,128)(2,1)}) %all-gather.27.cloned.1.call-update) | async-done | bytes 6291472 | tf_op jit(solution)/shard_map/all_gather | solution.py:80
  159.7 136.2 %all-gather.31.cloned.1.call-done = bf16[1,2048,2048]{2,1,0:T(8,128)(2,1)} async-done(((bf16[1,512,2048]{2,1,0:T(8,128)(2,1)}), bf16[1,2048,2048]{2,1,0:T(8,128)(2,1)}) %all-gather.31.cloned.1.call-update) | async-done | bytes 8388624 | tf_op jit(solution)/shard_map/all_gather | solution.py:81
  301.8 143.4 %all-gather.33.cloned.1.call-done = bf16[1,2048,2048]{2,1,0:T(8,128)(2,1)} async-done(((bf16[1,2048,512]{2,1,0:T(8,128)(2,1)}), bf16[1,2048,2048]{2,1,0:T(8,128)(2,1)}) %all-gather.33.cloned.1.call-update) | async-done | bytes 8388624 | tf_op jit(solution)/shard_map/all_gather | solution.py:85
  445.2 7.0 fusion.13
  452.2 38.2 %all-gather.29.cloned.1.call-done = bf16[1,512,2048]{2,1,0:T(8,128)(2,1)} async-done(((bf16[1,512,512]{2,1,0:T(8,128)(2,1)}), bf16[1,512,2048]{2,1,0:T(8,128)(2,1)}) %all-gather.29.cloned.1.call-update) | async-done | bytes 2097168 | tf_op jit(solution)/shard_map/all_gather | solution.py:84
  497.2 27.7 %reduce-scatter.8.cloned.1.call-done = f32[256,512]{1,0:T(8,128)} async-done(((f32[256,2048]{1,0:T(8,128)}), f32[256,512]{1,0:T(8,128)}) %reduce-scatter.8.cloned.1.call-update) | async-done | bytes 524304 | tf_op jit(solution)/shard_map/reduce_scatter | solution.py:120
  546.5 15.0 all-gather.17.cloned.1.call-done
  612.9 20.7 %reduce-scatter.10.cloned.1.call-done = f32[256,512]{1,0:T(8,128)} async-done(((f32[256,2048]{1,0:T(8,128)}), f32[256,512]{1,0:T(8,128)}) %reduce-scatter.10.cloned.1.call-update) | async-done | bytes 524304 | tf_op jit(solution)/shard_map/reduce_scatter | solution.py:120
  646.0 7.0 fusion.346
  654.0 7.1 fusion.19
  669.7 7.0 fusion.54
  688.4 62.9 %all-reduce.12.cloned.1.call-done = (f32[256,2048]{1,0:T(8,128)}, f32[256,2048]{1,0:T(8,128)}) async-done(((f32[256,2048]{1,0:T(8,128)}, f32[256,2048]{1,0:T(8,128)}), (f32[256,2048]{1,0:T(8,128)}, f32[256,2048]{1,0:T(8,128)})) %all-reduce.12.cloned.1.call-update) | async-done | bytes 4194320 | tf_op jit(solution)/shard_map/psum | solution.py:181
  759.1 7.2 collective-permute-done.2
  771.9 7.8 fusion.63
  802.7 7.5 fusion.345
  821.2 84.6 %all-reduce.10.cloned.1.call-done = (f32[256,2048]{1,0:T(8,128)}, f32[256,2048]{1,0:T(8,128)}) async-done(((f32[256,2048]{1,0:T(8,128)}, f32[256,2048]{1,0:T(8,128)}), (f32[256,2048]{1,0:T(8,128)}, f32[256,2048]{1,0:T(8,128)})) %all-reduce.10.cloned.1.call-update) | async-done | bytes 4194320 | tf_op jit(solution)/shard_map/psum | solution.py:181
  912.4 8.3 collective-permute-done.3
  931.4 7.1 all-gather.23.cloned.1.call-done
  956.1 6.7 fusion.27
  996.9 9.4 multiply_add_fusion.2
  1007.6 9.7 fusion.164
  1017.3 9.2 fusion.165
  1026.5 19.0 multiply_add_fusion.1
  1047.1 10.9 fusion.172
  1057.9 7.4 fusion.181
  1065.3 21.1 %multiply_add_fusion = f32[2048,2048]{1,0:T(8,128)} fusion(f32[2048,2048]{1,0:T(8,128)} %fusion.181, f32[2048,2048]{1,0:T(8,128)} %fusion.172, bf16[256,2048]{1,0:T(8,128)(2,1)} %all-gather.23.cloned.1.call-done, f32[]{:T(128)S(6)} %select_n.356, f32[]{:T(128)S(6)} %select_n.355, pred[]{:T(512)S(6)} %eq.3, f32[256,2048]{1,0:T(8,128)} %copy-done.13, ...), kind=kOutput, calls=%fused_computation.3 | convolution fusion | flops 2170028032 | bytes 55574536 | tf_op jit(solution)/shard_map/dot_general | solution.py:144
  1097.1 22.3 %all-reduce = (f32[1,1536]{1,0:T(1,128)}, f32[1,512]{1,0:T(1,128)}, f32[1,2048]{1,0:T(1,128)}, f32[1,2,2048]{2,1,0:T(2,128)}, f32[1,2,2048]{2,1,0:T(2,128)}) all-reduce(f32[1,1536]{1,0:T(1,128)S(1)} %broadcast_in_dim.55, f32[1,512]{1,0:T(1,128)S(1)} %bitcast.445, ...), channel_id=1, replica_groups=mesh['section'=2,'row'=4,'col'=4] {'col'}, use_global_device_ids=true, to_apply=%region_43.44 | all-reduce | flops 12288 | bytes 98304 | tf_op jit(solution)/shard_map/psum | solution.py:212
  1122.1 19.1 reduce-scatter.16.cloned.1.call-done
  1141.3 215.2 %reduce-scatter.14.cloned.1.call-done = f32[512,1536]{1,0:T(8,128)} async-done(((f32[2048,1536]{1,0:T(8,128)}), f32[512,1536]{1,0:T(8,128)}) %reduce-scatter.14.cloned.1.call-update) | async-done | bytes 3145744 | tf_op jit(solution)/shard_map/reduce_scatter | solution.py:205
  1356.5 284.4 %reduce-scatter.18.cloned.1.call-done = f32[512,2048]{1,0:T(8,128)} async-done(((f32[2048,2048]{1,0:T(8,128)}), f32[512,2048]{1,0:T(8,128)}) %reduce-scatter.18.cloned.1.call-update) | async-done | bytes 4194320 | tf_op jit(solution)/shard_map/reduce_scatter | solution.py:206
  1640.9 283.9 %reduce-scatter.20.cloned.1.call-done = f32[2048,512]{1,0:T(8,128)} async-done(((f32[2048,2048]{1,0:T(8,128)}), f32[2048,512]{1,0:T(8,128)}) %reduce-scatter.20.cloned.1.call-update) | async-done | bytes 4194320 | tf_op jit(solution)/shard_map/reduce_scatter | solution.py:210
  (616 shorter events, 273.5 us)
Async XLA Ops:
  7.2 22.4 %all-gather.25.cloned.1.call-start = ((), (), s32[]{:S(2)}) async-start(), calls=%async_computation.18 | async-start | bytes 1310720 | tf_op jit(solution)/shard_map/all_gather | solution.py:93
  8.9 137.6 %all-gather.27.cloned.1.call-start = ((), (), s32[]{:S(2)}) async-start(), calls=%async_computation.19 | async-start | bytes 7864320 | tf_op jit(solution)/shard_map/all_gather | solution.py:80
  9.7 286.2 %all-gather.31.cloned.1.call-start = ((), (), s32[]{:S(2)}) async-start(), calls=%async_computation.21 | async-start | bytes 10485760 | tf_op jit(solution)/shard_map/all_gather | solution.py:81
  10.5 434.7 %all-gather.33.cloned.1.call-start = ((), (), s32[]{:S(2)}) async-start(), calls=%async_computation.22 | async-start | bytes 10485760 | tf_op jit(solution)/shard_map/all_gather | solution.py:85
  11.0 479.4 %all-gather.29.cloned.1.call-start = ((), (), s32[]{:S(2)}) async-start(), calls=%async_computation.20 | async-start | bytes 2621440 | tf_op jit(solution)/shard_map/all_gather | solution.py:84
  11.6 513.3 %reduce-scatter.8.cloned.1.call-start = ((), (), s32[]{:S(2)}) async-start(), calls=%async_computation.7 | async-start | bytes 2621440 | tf_op jit(solution)/shard_map/reduce_scatter | solution.py:120
  14.3 143.0 %copy-start.89 = (f32[256,32]{1,0:T(8,128)}, f32[256,32]{1,0:T(8,128)S(1)}, u32[]{:S(2)}) copy-start(f32[256,32]{1,0:T(8,128)S(1)} %copy.208) | copy-start | bytes 98308
  158.4 137.5 %copy-start.115 = (f32[1,1,2048]{2,1,0:T(1,128)S(1)}, f32[1,1,2048]{2,1,0:T(1,128)}, u32[]{:S(2)}) copy-start(f32[1,1,2048]{2,1,0:T(1,128)} %get-tuple-element.160) | copy-start | bytes 24580
  158.4 137.5 %copy-start.164 = (f32[256]{0:T(256)S(1)}, f32[256]{0:T(256)}, u32[]{:S(2)}) copy-start(f32[256]{0:T(256)} %copy-done.163) | copy-start | bytes 3076
  158.5 137.5 %copy-start.171 = (f32[256]{0:T(256)S(1)}, f32[256]{0:T(256)}, u32[]{:S(2)}) copy-start(f32[256]{0:T(256)} %copy-done.170) | copy-start | bytes 3076
  158.5 137.5 %copy-start.174 = (f32[1,2048]{1,0:T(1,128)S(1)}, f32[1,2048]{1,0:T(1,128)}, u32[]{:S(2)}) copy-start(f32[1,2048]{1,0:T(1,128)} %param.23) | copy-start | bytes 24580
  159.0 137.0 %copy-start.59 = (bf16[256,2,256]{2,0,1:T(8,128)(2,1)}, bf16[256,2,256]{2,0,1:T(8,128)(2,1)S(1)}, u32[]{:S(2)}) copy-start(bf16[256,2,256]{2,0,1:T(8,128)(2,1)S(1)} %get-tuple-element.198) | copy-start | bytes 786436
  159.4 142.3 %copy-start.132 = (f32[2,256]{1,0:T(2,128)}, f32[2,256]{1,0:T(2,128)S(1)}, u32[]{:S(2)}) copy-start(f32[2,256]{1,0:T(2,128)S(1)} %log_add_fusion.2) | copy-start | bytes 6148
  301.7 150.5 %copy-start.9 = (f32[256,2048]{1,0:T(8,128)}, f32[256,2048]{1,0:T(8,128)S(1)}, u32[]{:S(2)}) copy-start(f32[256,2048]{1,0:T(8,128)S(1)} %fusion.57) | copy-start | bytes 6291460
  494.8 48.4 %all-gather.35.cloned.1.call-start = ((), (), s32[]{:S(2)}) async-start(), calls=%async_computation.23 | async-start | bytes 1310720 | tf_op jit(solution)/shard_map/all_gather | solution.py:134
  497.1 64.4 %all-gather.17.cloned.1.call-start = ((), (), s32[]{:S(2)}) async-start(), calls=%async_computation.8 | async-start | bytes 1310720 | tf_op jit(solution)/shard_map/all_gather | solution.py:93
  526.1 8.8 collective-permute-start
  535.6 98.0 %reduce-scatter.10.cloned.1.call-start = ((), (), s32[]{:S(2)}) async-start(), calls=%async_computation.9 | async-start | bytes 2621440 | tf_op jit(solution)/shard_map/reduce_scatter | solution.py:120
  602.2 60.6 %all-gather.19.cloned.1.call-start = ((), (), s32[]{:S(2)}) async-start(), calls=%async_computation.10 | async-start | bytes 1310720 | tf_op jit(solution)/shard_map/all_gather | solution.py:93
  635.4 9.8 collective-permute-start.1
  646.0 105.4 %all-reduce.12.cloned.1.call-start = ((), (), s32[]{:S(2)}) async-start(), calls=%async_computation.26 | async-start | bytes 8388608 | tf_op jit(solution)/shard_map/psum | solution.py:181
  661.1 123.0 %all-gather.21.cloned.1.call-start = ((), (), s32[]{:S(2)}) async-start(), calls=%async_computation.12 | async-start | bytes 1310720 | tf_op jit(solution)/shard_map/all_gather | solution.py:134
  756.6 9.7 collective-permute-start.2
  767.7 138.1 %all-reduce.10.cloned.1.call-start = ((), (), s32[]{:S(2)}) async-start(), calls=%async_computation.25 | async-start | bytes 8388608 | tf_op jit(solution)/shard_map/psum | solution.py:181
  820.1 118.4 %all-gather.23.cloned.1.call-start = ((), (), s32[]{:S(2)}) async-start(), calls=%async_computation.13 | async-start | bytes 1310720 | tf_op jit(solution)/shard_map/all_gather | solution.py:134
  911.1 9.6 collective-permute-start.3
  922.1 167.8 %reduce-scatter.12.cloned.1.call-start = ((), (), s32[]{:S(2)}) async-start(), calls=%async_computation.11 | async-start | bytes 2621440 | tf_op jit(solution)/shard_map/reduce_scatter | solution.py:120
  931.3 160.7 %all-reduce.8.cloned.1.call-start = ((), (), s32[]{:S(2)}) async-start(), calls=%async_computation.24 | async-start | bytes 8388608 | tf_op jit(solution)/shard_map/psum | solution.py:181
  974.3 167.0 %reduce-scatter.16.cloned.1.call-start = ((), (), s32[]{:S(2)}) async-start(), calls=%async_computation.15 | async-start | bytes 5242880 | tf_op jit(solution)/shard_map/reduce_scatter | solution.py:209
  985.3 371.1 %reduce-scatter.14.cloned.1.call-start = ((), (), s32[]{:S(2)}) async-start(), calls=%async_computation.14 | async-start | bytes 15728640 | tf_op jit(solution)/shard_map/reduce_scatter | solution.py:205
  1006.4 634.5 %reduce-scatter.18.cloned.1.call-start = ((), (), s32[]{:S(2)}) async-start(), calls=%async_computation.16 | async-start | bytes 20971520 | tf_op jit(solution)/shard_map/reduce_scatter | solution.py:206
  1045.5 879.3 %reduce-scatter.20.cloned.1.call-start = ((), (), s32[]{:S(2)}) async-start(), calls=%async_computation.17 | async-start | bytes 20971520 | tf_op jit(solution)/shard_map/reduce_scatter | solution.py:210
  (177 other events, 2178.6 us)
Sparse Core Ops, SparseCore 0:
  10.1 19.4 all-gather.24
  31.1 115.3 all-gather.26
  148.1 147.7 all-gather.30
  297.3 147.7 all-gather.32
  446.6 43.8 all-gather.28
  494.9 29.9 reduce-scatter.7
  526.5 16.6 all-gather.34
  544.8 16.6 all-gather.16
  602.3 31.1 reduce-scatter.9
  646.1 16.6 all-gather.18
  665.8 85.4 all-reduce.11
  767.8 16.2 all-gather.20
  820.2 85.4 all-reduce.9
  922.2 16.2 all-gather.22
  940.8 31.1 reduce-scatter.11
  974.4 85.5 all-reduce.7
  1062.7 78.4 reduce-scatter.15
  1144.0 212.3 reduce-scatter.13
  1359.4 281.4 reduce-scatter.17
  1643.7 281.0 reduce-scatter.19
where the time goes:
time: 1940 us; the launch traced here: 1930 us
  waiting for transfers between devices  1500 us (77%)
  matrix products  250 us (13%)
  local copies, waits for them, and re-layouts  67.8 us (3%)
  other arithmetic  61.7 us (3%)
  blocking collectives  22.3 us (1%)
    reduce_scatter x1, waiting for transfers between devices, reduce_grads(): lax.psum_scatter(weight_terms[1], 'col', scatter_dimension=0, tiled=True)  284 us
    reduce_scatter x1, waiting for transfers between devices, reduce_grads(): lax.psum_scatter(weight_terms[3], 'col', scatter_dimension=1, tiled=True)  284 us
    reduce_scatter x1, waiting for transfers between devices, reduce_grads(): lax.psum_scatter(weight_terms[0], 'col', scatter_dimension=0, tiled=True)  215 us
    psum x3, waiting for transfers between devices, backward_slot(): back_first, back_second = lax.psum((back_first, back_second), 'row')  148 us
    all_gather x1, waiting for transfers between devices, fetch_weights(): lax.all_gather(shards[3], 'col', axis=1, tiled=True)  143 us
    all_gather x1, waiting for transfers between devices, fetch_weights(): lax.all_gather(shards[1], 'col', axis=0, tiled=True)  136 us
    all_gather x1, waiting for transfers between devices, fetch_weights(): lax.all_gather(shards[0], 'col', axis=0, tiled=True)  114 us
    reduce_scatter x3, waiting for transfers between devices, forward_slot(): lax.psum_scatter(partial_sum, 'row', scatter_dimension=1, tiled=True)  48.4 us
  transfers between devices with their start and end apart: 24, of which 21 were waited for; matrix products, arithmetic and copies ran while one was open for 14% of the time, Pallas kernels for 0%

commit v1 on v0

v1 whole, which is shorter than its diff:
```python
import functools
import math

import jax
import jax.numpy as jnp
from jax import lax
from jax.experimental import pallas as pl
from jax.experimental.pallas import tpu as pltpu
from jax.sharding import PartitionSpec as P

HEAD_DIM = 256
ROT = 64
LEN = 256
NORM_EPS = 1e-05
BF16 = jnp.bfloat16
F32 = jnp.float32


def dot32(left, right):
    return jnp.dot(left, right, preferred_element_type=F32)


def dot_nt(left, right):
    return lax.dot_general(left, right, (((1,), (1,)), ((), ())), preferred_element_type=F32)


def dot_tn(left, right):
    return lax.dot_general(left, right, (((0,), (0,)), ((), ())), preferred_element_type=F32)


def rotary_tables(place_ids, rotary_dims):
    half_dims = rotary_dims // 2
    powers = jnp.arange(half_dims).astype(F32) * (2.0 / rotary_dims)
    inverse = jnp.exp(-math.log(10000.0) * powers)
    angles = place_ids.astype(F32)[:, None] * inverse[None, :]
    return (jnp.cos(angles), jnp.sin(angles))


def rotate_pairs(vectors, cosines, sines, direction):
    half_dims = ROT // 2
    lower = vectors[..., :half_dims]
    upper = vectors[..., half_dims:ROT]
    cos_part = cosines[:, None, :]
    sin_part = direction * sines[:, None, :]
    return jnp.concatenate(
        [
            lower * cos_part - upper * sin_part,
            upper * cos_part + lower * sin_part,
            vectors[..., ROT:],
        ],
        axis=-1,
    )


def gelu_parts(pre_act):
    cdf_value = 0.5 * (1.0 + lax.erf(pre_act * 0.5**0.5))
    density = jnp.exp(-0.5 * pre_act * pre_act) * (2.0 * math.pi) ** (-0.5)
    return (pre_act * cdf_value, cdf_value + pre_act * density)


def causal_scores(query_seq, key_seq):
    length = query_seq.shape[1]
    scores = jnp.einsum(
        "sqhd,skhd->shqk", query_seq, key_seq, preferred_element_type=F32
    ) * query_seq.shape[-1] ** (-0.5)
    allowed = jnp.arange(length)[:, None] >= jnp.arange(length)[None, :]
    return jnp.where(allowed, scores, -jnp.inf)


def half_of(array, axis, index, count):
    width = array.shape[axis] // count
    return lax.dynamic_slice_in_dim(array, index * width, width, axis)


def section_params(mine, other, section, layer):
    return jnp.where(section == layer, mine, other)


def spread_weight(shard, axis, section, sections, layer):
    own = half_of(shard, axis, section, sections)
    sent = half_of(shard, axis, 1 - section, sections)
    received = lax.ppermute(sent, "section", [(layer, 1 - layer)])
    return jnp.where(section == layer, own, received)


MESH = pl.DeviceIdType.MESH


def flipped(index, bit):
    return index + bit - 2 * bit * ((index // bit) % 2)


def greet(partners):
    barrier = pltpu.get_barrier_semaphore()
    for partner in partners:
        pl.semaphore_signal(barrier, inc=1, device_id=partner, device_id_type=MESH)
    pl.semaphore_wait(barrier, len(partners))


def peer_of(cols):
    return {"col": lax.rem(lax.axis_index("col") + cols // 2, cols)}


def row_bits(row_count):
    bits, bit = [], row_count // 2
    while bit >= 1:
        bits.append(bit)
        bit //= 2
    return bits


def gather_kernel(row_count, cols, chunks, block_ref, out_ref, send_sems, recv_sems, local_sem):
    me = lax.axis_index("row")
    rows, width = block_ref.shape
    bits = row_bits(row_count)
    peer = peer_of(cols)
    greet([peer] + [{"row": flipped(me, bit)} for bit in bits])
    step = rows // chunks
    started = []

    def columns(index):
        return pl.ds(pl.multiple_of(index * width, width), width)

    def send(source, target, partner):
        number = len(started)
        copy = pltpu.make_async_remote_copy(
            src_ref=source,
            dst_ref=target,
            send_sem=send_sems.at[number],
            recv_sem=recv_sems.at[number],
            device_id=partner,
            device_id_type=MESH,
        )
        copy.start()
        started.append(copy)
        return copy

    def spread(source_of, target_of, ready):
        ready()
        held = [(me, None)]
        for bit in bits:
            fresh = []
            for index, copy in held:
                if copy is not None:
                    copy.wait_recv()
                sent = send(source_of(index, copy), target_of(index), {"row": flipped(me, bit)})
                fresh.append((flipped(index, bit), sent))
            held = [(index, None) for index, _ in held] + fresh
        return held

    peer_copies = []
    for chunk in range(chunks):
        part = pl.ds(chunk * step, step)
        peer_copies.append(send(block_ref.at[part], out_ref.at[1, part, columns(me)], peer))
    local = pltpu.make_async_copy(block_ref, out_ref.at[0, :, columns(me)], local_sem)
    local.start()
    groups = []
    groups.append((0, pl.ds(0, rows), None))
    for chunk in range(chunks):
        groups.append((1, pl.ds(chunk * step, step), peer_copies[chunk]))
    held = []
    waited = set()
    state = []
    for place, part, arrival in groups:
        state.append([(me, arrival)])
    for bit in bits:
        for number, (place, part, _) in enumerate(groups):
            fresh = []
            for index, copy in state[number]:
                if copy is not None and id(copy) not in waited:
                    copy.wait_recv()
                    waited.add(id(copy))
                own = place == 0 and index is me
                source = block_ref if own else out_ref.at[place, part, columns(index)]
                sent = send(source, out_ref.at[place, part, columns(index)], {"row": flipped(me, bit)})
                fresh.append((flipped(index, bit), sent))
            state[number] = state[number] + fresh
    for copy in started:
        if id(copy) not in waited:
            copy.wait_recv()
        copy.wait_send()
    local.wait()


def gather_rows(block):
    row_count, cols = lax.axis_size("row"), lax.axis_size("col")
    rows, width = block.shape
    chunks = 2
    copies = chunks + (chunks + 1) * (row_count - 1)
    return pl.pallas_call(
        functools.partial(gather_kernel, row_count, cols, chunks),
        out_shape=jax.ShapeDtypeStruct((2, rows, row_count * width), block.dtype),
        in_specs=[pl.BlockSpec(memory_space=pltpu.VMEM)],
        out_specs=pl.BlockSpec(memory_space=pl.ANY),
        scratch_shapes=[
            pltpu.SemaphoreType.DMA((copies,)),
            pltpu.SemaphoreType.DMA((copies,)),
            pltpu.SemaphoreType.DMA,
        ],
        compiler_params=pltpu.CompilerParams(collective_id=1, has_side_effects=True),
        name="gather_rows",
    )(block)


def reduce_kernel(row_count, cols, chunks, with_peer, *refs):
    count = len(with_peer)
    ins = sum(2 if both else 1 for both in with_peer)
    in_refs, refs = refs[:ins], refs[ins:]
    out_refs, refs = refs[:count], refs[count:]
    first_buf, first_send, pair_buf, pair_send, last_buf, last_send, send_sems, recv_sems = refs
    me = lax.axis_index("row")
    section = lax.axis_index("section")
    rows, features = in_refs[0].shape
    width = features // row_count
    bits = row_bits(row_count)[::-1]
    peer = peer_of(cols)
    other = {"section": 1 - section}
    greet([peer, other] + [{"row": flipped(me, bit)} for bit in bits])
    step = rows // chunks
    started = []

    def columns(index):
        return pl.ds(pl.multiple_of(index * width, width), width)

    def send(source, target, partner):
        number = len(started)
        copy = pltpu.make_async_remote_copy(
            src_ref=source,
            dst_ref=target,
            send_sem=send_sems.at[number],
            recv_sem=recv_sems.at[number],
            device_id=partner,
            device_id_type=MESH,
        )
        copy.start()
        started.append(copy)
        return copy

    own_slots, items, slot = [], [], 0
    for output, both in enumerate(with_peer):
        own_slots.append(slot)
        if both:
            for chunk in range(chunks):
                items.append((slot + 1, chunk, output, True))
        slot += 2 if both else 1
    for output, both in enumerate(with_peer):
        for chunk in range(chunks):
            items.append((own_slots[output], chunk, output, False))

    def subsets(low_bits):
        masks = [[]]
        for bit in low_bits:
            masks = masks + [mask + [bit] for mask in masks]
        return masks

    def moved(index, mask):
        for bit in mask:
            index = flipped(index, bit)
        return index

    pending = []
    for slot, chunk, output, is_peer in items:
        part = pl.ds(chunk * step, step)
        partner = flipped(me, bits[0])
        copies = []
        for number, mask in enumerate(subsets(bits[1:])):
            copies.append(
                send(
                    in_refs[slot].at[part, columns(moved(partner, mask))],
                    first_buf.at[slot, number, part],
                    {"row": partner},
                )
            )
        pending.append(copies)
    sums = []
    for (slot, chunk, output, is_peer), copies in zip(items, pending):
        part = pl.ds(chunk * step, step)
        held = []
        for number, mask in enumerate(subsets(bits[1:])):
            copies[number].wait_recv()
            held.append(
                (
                    mask,
                    in_refs[slot][part, columns(moved(me, mask))].astype(F32)
                    + first_buf[slot, number, part].astype(F32),
                )
            )
        sums.append(held)
        if len(bits) > 1:
            kept = []
            sent = []
            for mask, value in held:
                if bits[1] in mask:
                    first_send[slot, part] = value.astype(BF16)
                    sent.append(
                        send(first_send.at[slot, part], pair_buf.at[slot, part], {"row": flipped(me, bits[1])})
                    )
                else:
                    pair_send[slot, part] = value
            pending[items.index((slot, chunk, output, is_peer))] = sent
    peers = {}
    lasts = {}
    for (slot, chunk, output, is_peer), copies in zip(items, pending):
        part = pl.ds(chunk * step, step)
        copies[0].wait_recv()
        value = pair_send[slot, part] + pair_buf[slot, part].astype(F32)
        if is_peer:
            last_send[slot, part] = value.astype(BF16)
            peers[(output, chunk)] = (
                slot,
                send(last_send.at[slot, part], last_buf.at[slot, part], peer),
            )
        else:
            if (output, chunk) in peers:
                peer_slot, copy = peers[(output, chunk)]
                copy.wait_recv()
                value = value + last_buf[peer_slot, part].astype(F32)
            last_send[slot, part] = value.astype(BF16)
            lasts[(output, chunk)] = (
                slot,
                send(last_send.at[slot, part], last_buf.at[slot, part], other),
            )
    for (output, chunk), (slot, copy) in lasts.items():
        part = pl.ds(chunk * step, step)
        copy.wait_recv()
        out_refs[output][part] = last_send[slot, part].astype(F32) + last_buf[slot, part].astype(F32)
    for copy in started:
        copy.wait_send()


def reduce_rows(pairs, collective_id):
    row_count, cols = lax.axis_size("row"), lax.axis_size("col")
    assert row_count == 4
    rows, features = pairs[0][0].shape
    width = features // row_count
    with_peer = tuple(peer is not None for _, peer in pairs)
    operands = [member for pair in pairs for member in pair if member is not None]
    slots = len(operands)
    chunks = 4
    copies = slots * chunks * (row_count // 2 + 1 + 1)
    return pl.pallas_call(
        functools.partial(reduce_kernel, row_count, cols, chunks, with_peer),
        out_shape=[jax.ShapeDtypeStruct((rows, width), F32) for _ in pairs],
        in_specs=[pl.BlockSpec(memory_space=pltpu.VMEM)] * slots,
        out_specs=[pl.BlockSpec(memory_space=pltpu.VMEM)] * len(pairs),
        scratch_shapes=[
            pltpu.VMEM((slots, row_count // 2, rows, width), BF16),
            pltpu.VMEM((slots, rows, width), BF16),
            pltpu.VMEM((slots, rows, width), BF16),
            pltpu.VMEM((slots, rows, width), F32),
            pltpu.VMEM((slots, rows, width), BF16),
            pltpu.VMEM((slots, rows, width), BF16),
            pltpu.SemaphoreType.DMA((copies,)),
            pltpu.SemaphoreType.DMA((copies,)),
        ],
        compiler_params=pltpu.CompilerParams(collective_id=collective_id, has_side_effects=True),
        name="reduce_rows",
    )(*operands)


def stats_kernel(row_count, in_ref, out_ref, buf, send, send_sems, recv_sems):
    me = lax.axis_index("row")
    bits = row_bits(row_count)
    greet([{"row": flipped(me, bit)} for bit in bits])
    value = in_ref[...]
    for number, bit in enumerate(bits):
        send[number] = value
        copy = pltpu.make_async_remote_copy(
            src_ref=send.at[number],
            dst_ref=buf.at[number],
            send_sem=send_sems.at[number],
            recv_sem=recv_sems.at[number],
            device_id={"row": flipped(me, bit)},
            device_id_type=MESH,
        )
        copy.start()
        copy.wait()
        value = value + buf[number]
    out_ref[...] = value


def row_sum(stats):
    row_count = lax.axis_size("row")
    stages = len(row_bits(row_count))
    return pl.pallas_call(
        functools.partial(stats_kernel, row_count),
        out_shape=jax.ShapeDtypeStruct(stats.shape, F32),
        in_specs=[pl.BlockSpec(memory_space=pltpu.VMEM)],
        out_specs=pl.BlockSpec(memory_space=pltpu.VMEM),
        scratch_shapes=[
            pltpu.VMEM((stages,) + stats.shape, F32),
            pltpu.VMEM((stages,) + stats.shape, F32),
            pltpu.SemaphoreType.DMA((stages,)),
            pltpu.SemaphoreType.DMA((stages,)),
        ],
        compiler_params=pltpu.CompilerParams(collective_id=4, has_side_effects=True),
        name="row_sum",
    )(stats)


def layer_forward(entry, params, weights, tables):
    gains, shifts, b_qkv, b_fc1, b_out = params
    w_qkv, w_fc1, w_dense, w_fc2 = weights
    cosines, sines = tables
    rows = entry.shape[0]
    field = gather_rows(entry).reshape(2 * rows, -1).astype(F32)
    center = field - jnp.mean(field, axis=-1, keepdims=True)
    rstd = lax.rsqrt(jnp.mean(center * center, axis=-1, keepdims=True) + NORM_EPS)
    normed = center * rstd
    first_low = (normed[:rows] * gains[0] + shifts[0]).astype(BF16)
    second_low = (normed * gains[1] + shifts[1]).astype(BF16)
    heads = w_qkv.shape[1] // (3 * HEAD_DIM)
    mixed = (dot32(first_low, w_qkv) + b_qkv).reshape(rows, heads, 3, HEAD_DIM)
    query = rotate_pairs(mixed[:, :, 0], cosines, sines, 1.0).astype(BF16)
    keys = rotate_pairs(mixed[:, :, 1], cosines, sines, 1.0).astype(BF16)
    values = mixed[:, :, 2].astype(BF16)
    seq = (rows // LEN, LEN, heads, HEAD_DIM)
    scores = causal_scores(query.reshape(seq), keys.reshape(seq))
    top = jnp.max(scores, axis=-1, keepdims=True)
    logsum = top + jnp.log(jnp.sum(jnp.exp(scores - top), axis=-1, keepdims=True))
    probs = jnp.exp(scores - logsum).astype(BF16)
    attended = jnp.einsum("shqk,skhd->sqhd", probs, values.reshape(seq), preferred_element_type=F32)
    attn_out = attended.reshape(rows, heads * HEAD_DIM).astype(BF16)
    pre_act = dot32(second_low, w_fc1) + b_fc1
    activation = gelu_parts(pre_act)[0].astype(BF16)
    own = (dot32(attn_out, w_dense) + dot32(activation[:rows], w_fc2)).astype(BF16)
    peers = dot32(activation[rows:], w_fc2).astype(BF16)
    (summed,) = reduce_rows([(own, peers)], 2)
    output = (entry.astype(F32) + summed + b_out).astype(BF16)
    return output, (center[:rows], rstd[:rows], first_low, second_low, query, keys, values, attn_out, logsum, pre_act, activation)


def layer_backward(grad, wide_grad, saved, params, weights, tables):
    gains = params[0]
    w_qkv, w_fc1, w_dense, w_fc2 = weights
    cosines, sines = tables
    center, rstd, first_low, second_low, query, keys, values, attn_out, logsum, pre_act, activation = saved
    rows, width = grad.shape
    wide_own = wide_grad[0]
    wide_grad = wide_grad.reshape(2 * rows, -1)
    g_fc2 = dot_tn(activation, wide_grad).astype(BF16)
    g_dense = dot_tn(attn_out, wide_own).astype(BF16)
    d_pre = dot_nt(wide_grad, w_fc2) * gelu_parts(pre_act)[1]
    d_pre_low = d_pre.astype(BF16)
    g_fc1 = dot_tn(second_low, d_pre_low).astype(BF16)
    d_attn = dot_nt(wide_own, w_dense).astype(BF16)
    heads = w_qkv.shape[1] // (3 * HEAD_DIM)
    seq = (rows // LEN, LEN, heads, HEAD_DIM)
    head_shape = (rows, heads, HEAD_DIM)
    query_seq, key_seq = query.reshape(seq), keys.reshape(seq)
    grad_seq = d_attn.reshape(seq)
    probs = jnp.exp(causal_scores(query_seq, key_seq) - logsum)
    d_values = jnp.einsum("shqk,sqhd->skhd", probs.astype(BF16), grad_seq, preferred_element_type=F32)
    d_probs = jnp.einsum("sqhd,skhd->shqk", grad_seq, values.reshape(seq), preferred_element_type=F32)
    row_dots = jnp.einsum("sqhd,sqhd->shq", grad_seq, attn_out.reshape(seq), preferred_element_type=F32)[..., None]
    d_scores = (probs * (d_probs - row_dots) * HEAD_DIM ** (-0.5)).astype(BF16)
    d_query = jnp.einsum("shqk,skhd->sqhd", d_scores, key_seq, preferred_element_type=F32).reshape(head_shape)
    d_keys = jnp.einsum("shqk,sqhd->skhd", d_scores, query_seq, preferred_element_type=F32).reshape(head_shape)
    d_query = rotate_pairs(d_query, cosines, sines, -1.0)
    d_keys = rotate_pairs(d_keys, cosines, sines, -1.0)
    d_mixed = jnp.stack([d_query, d_keys, d_values.reshape(head_shape)], axis=2).reshape(rows, 3 * heads * HEAD_DIM)
    d_mixed_low = d_mixed.astype(BF16)
    g_qkv = dot_tn(first_low, d_mixed_low).astype(BF16)
    back_first = dot_nt(d_mixed_low, w_qkv).astype(BF16)
    back_second = dot_nt(d_pre_low, w_fc1).astype(BF16)
    totals = reduce_rows([(back_first, None), (back_second[:rows], back_second[rows:])], 3)
    row_index = lax.axis_index("row")
    row_count = lax.axis_size("row")
    my_normed = half_of(center, 1, row_index, row_count) * rstd
    my_gains = half_of(gains, 1, row_index, row_count)
    sums = []
    for total, my_gain in zip(totals, my_gains):
        scaled = total * my_gain
        sums.append(jnp.sum(scaled, axis=-1))
        sums.append(jnp.sum(scaled * my_normed, axis=-1))
    stats = row_sum(jnp.stack(sums + sums)) / (row_count * width)
    d_input = grad.astype(F32)
    gain_terms, shift_terms = [], []
    for index, total in enumerate(totals):
        d_input = d_input + rstd * (
            total * my_gains[index] - stats[2 * index][:, None] - my_normed * stats[2 * index + 1][:, None]
        )
        gain_terms.append(jnp.sum(total * my_normed, axis=0))
        shift_terms.append(jnp.sum(total, axis=0))
    small = (
        jnp.stack(gain_terms + shift_terms),
        jnp.sum(d_mixed, axis=0),
        jnp.sum(d_pre, axis=0),
        jnp.sum(grad.astype(F32), axis=0),
    )
    return d_input, (g_qkv, g_fc1, g_dense, g_fc2), small


AXES = (1, 1, 0, 0)


def halves_of(cols):
    group = cols // 2
    return [list(range(group)), list(range(group, cols))]


def peer_pairs(cols):
    return [(index, (index + cols // 2) % cols) for index in range(cols)]


def gather_hidden(part, axis, half, cols):
    other = 1 - axis
    own = half_of(part, axis, half, 2)
    received = lax.ppermute(half_of(part, axis, 1 - half, 2), "col", peer_pairs(cols))
    stacked = jnp.stack([jnp.where(half == 0, own, received), jnp.where(half == 0, received, own)])
    wide = lax.all_gather(stacked, "col", axis=0, axis_index_groups=halves_of(cols))
    if other == 0:
        return wide.transpose(1, 0, 2, 3).reshape(cols * own.shape[0], own.shape[1])
    return wide.transpose(2, 1, 0, 3).reshape(own.shape[0], cols * own.shape[1])


def scatter_hidden(grad, axis, half, cols):
    group = cols // 2
    if axis == 1:
        stacked = grad.reshape(2, group, grad.shape[0] // cols, grad.shape[1]).transpose(1, 0, 2, 3)
    else:
        stacked = grad.reshape(grad.shape[0], 2, group, grad.shape[1] // cols).transpose(2, 1, 0, 3)
    mine = lax.psum_scatter(stacked, "col", scatter_dimension=0, axis_index_groups=halves_of(cols))
    own = jnp.where(half == 0, mine[0], mine[1])
    received = lax.ppermute(jnp.where(half == 0, mine[1], mine[0]), "col", peer_pairs(cols))
    return jnp.concatenate([jnp.where(half == 0, own, received), jnp.where(half == 0, received, own)], axis=axis)


def scatter_grads(grads, half, cols):
    g_qkv, g_fc1, g_dense, g_fc2 = grads
    return (
        lax.psum_scatter(g_qkv, "col", scatter_dimension=0, tiled=True),
        scatter_hidden(g_fc1, 1, half, cols),
        lax.psum_scatter(g_dense, "col", scatter_dimension=1, tiled=True),
        scatter_hidden(g_fc2, 0, half, cols),
    )


def local(
    inputs,
    positions,
    cotangent,
    norm_gains,
    norm_biases,
    qkv_weight,
    qkv_bias,
    dense_weight,
    dense_bias,
    fc1_weight,
    fc1_bias,
    fc2_weight,
    fc2_bias,
):
    sections = lax.axis_size("section")
    section = lax.axis_index("section")
    cols = lax.axis_size("col")
    half = lax.axis_index("col") // (cols // 2)
    micro, tokens, width = inputs.shape
    rows = micro * tokens
    shards = (qkv_weight[0], fc1_weight[0], dense_weight[0], fc2_weight[0])

    own = (norm_gains[0], norm_biases[0], qkv_bias[0], fc1_bias[0], dense_bias[0] + fc2_bias[0])
    packed = jnp.concatenate([member.reshape(-1) for member in own])
    theirs = lax.ppermute(packed, "section", [(0, 1), (1, 0)])
    layer_params = []
    for layer in range(sections):
        flat = section_params(packed, theirs, section, layer)
        members, start = [], 0
        for member in own:
            members.append(flat[start : start + member.size].reshape(member.shape))
            start += member.size
        gains, shifts, b_qkv, b_fc1, b_out = members
        layer_params.append(
            (gains, shifts, half_of(b_qkv, 0, section, sections), half_of(b_fc1, 0, 2 * section + half, 2 * sections), b_out)
        )

    tables = rotary_tables(positions.reshape(rows), ROT)
    weights = []
    for layer in range(sections):
        parts = [spread_weight(shard, axis, section, sections, layer) for shard, axis in zip(shards, AXES)]
        weights.append(
            (
                lax.all_gather(parts[0], "col", axis=0, tiled=True),
                gather_hidden(parts[1], 1, half, cols),
                lax.all_gather(parts[2], "col", axis=1, tiled=True),
                gather_hidden(parts[3], 0, half, cols),
            )
        )

    entry = inputs.reshape(rows, width)
    outputs, saves = [], []
    for layer in range(sections):
        entry, saved = layer_forward(entry, layer_params[layer], weights[layer], tables)
        outputs.append(entry)
        saves.append(saved)

    grad = cotangent.reshape(rows, width)
    input_grads, part_grads, returned, smalls = [None] * sections, [None] * sections, [None] * sections, [None] * sections
    for layer in reversed(range(sections)):
        wide_grad = gather_rows(grad)
        d_input, grads, small = layer_backward(
            grad, wide_grad, saves[layer], layer_params[layer], weights[layer], tables
        )
        input_grads[layer] = d_input
        grad = d_input.astype(BF16)
        part_grads[layer] = scatter_grads(grads, half, cols)
        returned[layer] = tuple(
            lax.ppermute(member, "section", [(1 - layer, layer)]) for member in part_grads[layer]
        )
        hidden_term = jnp.where(jnp.arange(2)[:, None] == half, small[2][None], 0.0).reshape(-1)
        smalls[layer] = small[:2] + (hidden_term,) + small[3:]

    first = section == 0

    def pick(values):
        return jnp.where(first, values[0], values[1])

    weight_grads = []
    for index, axis in enumerate(AXES):
        mine = pick([part_grads[layer][index] for layer in range(sections)]).astype(F32)
        other = pick([returned[layer][index] for layer in range(sections)]).astype(F32)
        weight_grads.append(
            jnp.concatenate([jnp.where(first, mine, other), jnp.where(first, other, mine)], axis=axis)[None]
        )

    norm_terms = pick([smalls[layer][0] for layer in range(sections)])
    out_term = pick([smalls[layer][3] for layer in range(sections)])
    bias_mine = pick([jnp.concatenate([smalls[layer][1], smalls[layer][2]]) for layer in range(sections)])
    bias_sent = pick([jnp.concatenate([smalls[layer][1], smalls[layer][2]]) for layer in reversed(range(sections))])
    bias_other = lax.ppermute(bias_sent, "section", [(0, 1), (1, 0)])
    summed = lax.psum(jnp.concatenate([norm_terms.reshape(-1), out_term, bias_mine, bias_other]), "col")
    count = norm_terms.size
    norm_sums = lax.all_gather(summed[:count].reshape(4, width), "row", axis=1, tiled=True)
    out_bias_grad = summed[count : count + width]
    qkv_size = smalls[0][1].size
    fc1_size = smalls[0][2].size
    mine = summed[count + width : count + width + qkv_size + fc1_size]
    other = summed[count + width + qkv_size + fc1_size :]
    lower = jnp.where(first, mine, other)
    upper = jnp.where(first, other, mine)
    qkv_bias_grad = jnp.concatenate([lower[:qkv_size], upper[:qkv_size]])
    fc1_bias_grad = jnp.concatenate([lower[qkv_size:], upper[qkv_size:]])
    shape = (1, micro, tokens, width)
    return (
        pick(outputs).reshape(shape),
        pick(input_grads).reshape(shape),
        weight_grads[0],
        qkv_bias_grad[None],
        weight_grads[2],
        out_bias_grad[None],
        weight_grads[1],
        fc1_bias_grad[None],
        weight_grads[3],
        norm_sums[None, :2],
        norm_sums[None, 2:],
    )


def solution(mesh):
    in_specs = (
        P(None, "col", "row"),
        P(None, "col"),
        P(None, "col", "row"),
        P("section", None, None),
        P("section", None, None),
        P("section", "col", "row"),
        P("section", "row"),
        P("section", "row", "col"),
        P("section", "row"),
        P("section", "col", "row"),
        P("section", "row"),
        P("section", "row", "col"),
        P("section", "row"),
    )
    out_specs = (
        P("section", None, "col", "row"),
        P("section", None, "col", "row"),
        P("section", "col", "row"),
        P("section", "row"),
        P("section", "row", "col"),
        P("section", "row"),
        P("section", "col", "row"),
        P("section", "row"),
        P("section", "row", "col"),
        P("section", None, None),
        P("section", None, None),
    )
    return jax.shard_map(local, mesh=mesh, in_specs=in_specs, out_specs=out_specs, check_vma=False)
```

time: 1940 us -> 1150 us (0.59)
  waiting for transfers between devices: 1500 us -> 303 us
  Pallas kernels: 0 us -> 404 us
  matrix products: 250 us -> 121 us
  starting transfers between devices: 12 us -> 73.9 us
  local copies, waits for them, and re-layouts: 67.8 us -> 110 us
  other arithmetic: 61.7 us -> 91.5 us
    reduce_scatter x7 -> x8, waiting for transfers between devices: 851 us -> 0.05 us  [the longest x4 0.03 us: scatter_hidden(): lax.psum_scatter(stacked, 'col', scatter_dimension=0, axis_index_groups=h...]
    all_gather x10 -> x8, waiting for transfers between devices: 479 us -> 21.4 us  [the longest x2 16.3 us: local(): lax.all_gather(parts[0], 'col', axis=0, tiled=True)]
    pallas_call x0 -> x10, Pallas kernels: none -> 404 us  [the longest x4 244 us: reduce_rows(): pl.pallas_call(functools.partial(reduce_kernel, row_count, cols, chunks,...]
    ppermute x4 -> x26, waiting for transfers between devices: 20.9 us -> 281 us  [the longest x4 111 us: scatter_hidden(): lax.ppermute(jnp.where(half == 0, mine[1], mine[0]), 'col', peer_pairs(co...]
    psum x3 -> x0, waiting for transfers between devices: 148 us -> none  [backward_slot(): back_first, back_second = lax.psum((back_first, back_second), 'row')]
    dot_general x51 -> x36, matrix products: 248 us -> 118 us  [the longest x10 41.7 us: dot32(): return jnp.dot(left, right, preferred_element_type=F32)]
    ppermute x4 -> x26, starting transfers between devices: 9.48 us -> 62 us  [the longest x8 28 us: spread_weight(): received = lax.ppermute(sent, 'section', [(layer, 1 - layer)])]
    select_n x6 -> x22, other arithmetic: 4.33 us -> 24.2 us  [the longest x4 6.66 us: scatter_hidden(): jnp.where(half == 0, mine[1], mine[0])]
  transfers between devices with their start and end apart: 24 -> 42, of which waited for: 21 -> 19; matrix products, arithmetic and copies ran while one was open for 14% -> 22% of each run, Pallas kernels for 0% -> 35%
where the time goes in v1:
time: 1150 us; the launch traced here: 1140 us
  Pallas kernels  404 us (35%)
  waiting for transfers between devices  303 us (26%)
  matrix products  121 us (11%)
  local copies, waits for them, and re-layouts  110 us (10%)
  other arithmetic  91.5 us (8%)
  starting transfers between devices  73.9 us (6%)
  blocking collectives  21 us (2%)
  between operations  16.5 us (1%)
    pallas_call x4, Pallas kernels, reduce_rows(): pl.pallas_call(functools.partial(reduce_kernel, row_count, cols, chunks,...  244 us
    pallas_call x4, Pallas kernels, gather_rows(): pl.pallas_call(functools.partial(gather_kernel, row_count, cols, chunks),...  148 us
    ppermute x4, waiting for transfers between devices, scatter_hidden(): lax.ppermute(jnp.where(half == 0, mine[1], mine[0]), 'col', peer_pairs(co...  111 us
    ppermute x4, waiting for transfers between devices, gather_hidden(): lax.ppermute(half_of(part, axis, 1 - half, 2), 'col', peer_pairs(cols))  98.5 us
    dot_general x10, matrix products, dot32(): return jnp.dot(left, right, preferred_element_type=F32)  41.7 us
    dot_general x8, matrix products, dot_tn(): lax.dot_general(left, right, (((0,), (0,)), ((), ())), preferred_element_...  38.6 us
    ppermute x8, waiting for transfers between devices, spread_weight(): received = lax.ppermute(sent, 'section', [(layer, 1 - layer)])  36.7 us
    ppermute x8, waiting for transfers between devices, local(): lax.ppermute(member, 'section', [(1 - layer, layer)])  35 us
  transfers between devices with their start and end apart: 42, of which 19 were waited for; matrix products, arithmetic and copies ran while one was open for 22% of the time, Pallas kernels for 35%

profile of v1, /device:TPU:0, one launch (start us, length us, event | category | flops | bytes accessed | tf_op | source)
XLA Modules:
  0.0 1140.7 jit_solution(11264877985508583288)
XLA Ops:
  21.7 19.9 %collective-permute-done.8 = bf16[256,512]{1,0:T(8,128)(2,1)S(1)} collective-permute-done((bf16[256,512]{1,0:T(8,128)(2,1)S(1)}, bf16[256,512]{1,0:T(8,128)(2,1)S(1)}, u32[]{:S(2)}, u32[]{:S(2)}) %collective-permute-start.8) | collective-permute-done | bytes 262176 | tf_op jit(solution)/shard_map/ppermute | solution.py:82
  51.6 6.7 collective-permute-start.3
  58.3 29.9 %collective-permute-done.6 = bf16[512,512]{1,0:T(8,128)(2,1)S(1)} collective-permute-done((bf16[512,512]{1,0:T(8,128)(2,1)S(1)}, bf16[512,512]{1,0:T(8,128)(2,1)S(1)}, u32[]{:S(2)}, u32[]{:S(2)}) %collective-permute-start.6) | collective-permute-done | bytes 524320 | tf_op jit(solution)/shard_map/ppermute | solution.py:509
  95.5 31.5 %collective-permute-done.4 = bf16[512,512]{1,0:T(8,128)(2,1)S(1)} collective-permute-done((bf16[512,512]{1,0:T(8,128)(2,1)S(1)}, bf16[512,512]{1,0:T(8,128)(2,1)S(1)}, u32[]{:S(2)}, u32[]{:S(2)}) %collective-permute-start.4) | collective-permute-done | bytes 524320 | tf_op jit(solution)/shard_map/ppermute | solution.py:509
  127.0 13.0 %collective-permute-done.10 = bf16[512,512]{1,0:T(8,128)(2,1)S(1)} collective-permute-done((bf16[512,512]{1,0:T(8,128)(2,1)S(1)}, bf16[512,512]{1,0:T(8,128)(2,1)S(1)}, u32[]{:S(2)}, u32[]{:S(2)}) %collective-permute-start.10) | collective-permute-done | bytes 524320 | tf_op jit(solution)/shard_map/ppermute | solution.py:509
  141.8 24.2 %collective-permute-done.12 = bf16[512,512]{1,0:T(8,128)(2,1)S(1)} collective-permute-done((bf16[512,512]{1,0:T(8,128)(2,1)S(1)}, bf16[512,512]{1,0:T(8,128)(2,1)S(1)}, u32[]{:S(2)}, u32[]{:S(2)}) %collective-permute-start.12) | collective-permute-done | bytes 524320 | tf_op jit(solution)/shard_map/ppermute | solution.py:509
  176.7 14.3 %collective-permute-done.7 = bf16[512,768]{1,0:T(8,128)(2,1)S(1)} collective-permute-done((bf16[512,768]{1,0:T(8,128)(2,1)S(1)}, bf16[512,768]{1,0:T(8,128)(2,1)S(1)}, u32[]{:S(2)}, u32[]{:S(2)}) %collective-permute-start.7) | collective-permute-done | bytes 786464 | tf_op jit(solution)/shard_map/ppermute | solution.py:82
  197.9 33.5 %gather_rows.4 = bf16[2,512,2048]{2,1,0:T(8,128)(2,1)} custom-call(bf16[512,512]{1,0:T(8,128)(2,1)} %bitcast.374), custom_call_target="tpu_custom_call" | custom-call | tf_op jit(solution)/shard_map/gather_rows/pallas_call | solution.py:190
  236.7 6.6 bitcast_subtract_fusion.1
  243.3 38.8 %gather_rows.6 = bf16[2,512,2048]{2,1,0:T(8,128)(2,1)} custom-call(bf16[512,512]{1,0:T(8,128)(2,1)} %bitcast.360), custom_call_target="tpu_custom_call" | custom-call | tf_op jit(solution)/shard_map/gather_rows/pallas_call | solution.py:190
  290.4 10.5 reduce-scatter.15.cloned.1.call-start
  327.8 16.3 %all-gather.13.cloned.1.call-done = bf16[2048,768]{1,0:T(8,128)(2,1)} async-done(((bf16[512,768]{1,0:T(8,128)(2,1)}), bf16[2048,768]{1,0:T(8,128)(2,1)}) %all-gather.13.cloned.1.call-update) | async-done | bytes 3145744 | tf_op jit(solution)/shard_map/all_gather | solution.py:583
  344.0 6.1 convolution_add_fusion.1
  376.8 72.5 %reduce_rows.4 = f32[512,512]{1,0:T(8,128)} custom-call(bf16[512,2048]{1,0:T(8,128)(2,1)} %add_convert_fusion.7.refs_0_, bf16[512,2048]{1,0:T(8,128)(2,1)} %convolution_convert_fusion.9.refs_1_), custom_call_target="tpu_custom_call" | custom-call | tf_op jit(solution)/shard_map/reduce_rows/pallas_call | solution.py:341
  451.6 39.4 %gather_rows.5 = bf16[2,512,2048]{2,1,0:T(8,128)(2,1)} custom-call(bf16[512,512]{1,0:T(8,128)(2,1)} %add_convert_fusion.13.block_ref), custom_call_target="tpu_custom_call" | custom-call | tf_op jit(solution)/shard_map/gather_rows/pallas_call | solution.py:190
  496.3 7.0 bitcast_subtract_fusion
  503.3 6.1 convolution_add_fusion
  570.0 48.4 %reduce_rows.6 = (f32[512,512]{1,0:T(8,128)}, f32[512,512]{1,0:T(8,128)}) custom-call(bf16[512,2048]{1,0:T(8,128)(2,1)} %convolution_convert_fusion.7.refs_0_, bf16[512,2048]{1,0:T(8,128)(2,1)} %get-tuple-element.53.refs_1_, bf16[512,2048]{1,0:T(8,128)(2,1)} %get-tuple-element.52.refs_2_), custom_call_target="tpu_custom_call" | custom-call | tf_op jit(solution)/shard_map/reduce_rows/pallas_call | solution.py:341
  622.5 5.9 row_sum.2
  633.0 36.4 %gather_rows.7 = bf16[2,512,2048]{2,1,0:T(8,128)(2,1)} custom-call(bf16[512,512]{1,0:T(8,128)(2,1)} %get-tuple-element.40.block_ref), custom_call_target="tpu_custom_call" | custom-call | tf_op jit(solution)/shard_map/gather_rows/pallas_call | solution.py:190
  684.1 6.1 fusion.10
  706.0 6.1 fusion.159
  712.1 6.3 fusion.11
  771.1 48.4 %reduce_rows.7 = (f32[512,512]{1,0:T(8,128)}, f32[512,512]{1,0:T(8,128)}) custom-call(bf16[512,2048]{1,0:T(8,128)(2,1)} %convolution_convert_fusion.6.refs_0_, bf16[512,2048]{1,0:T(8,128)(2,1)} %get-tuple-element.51.refs_1_, bf16[512,2048]{1,0:T(8,128)(2,1)} %get-tuple-element.50.refs_2_), custom_call_target="tpu_custom_call" | custom-call | tf_op jit(solution)/shard_map/reduce_rows/pallas_call | solution.py:341
  827.0 5.9 row_sum.3
  836.6 74.7 %reduce_rows.5 = f32[512,512]{1,0:T(8,128)} custom-call(bf16[512,2048]{1,0:T(8,128)(2,1)} %add_convert_fusion.6.refs_0_, bf16[512,2048]{1,0:T(8,128)(2,1)} %convolution_convert_fusion.8.refs_1_), custom_call_target="tpu_custom_call" | custom-call | tf_op jit(solution)/shard_map/reduce_rows/pallas_call | solution.py:341
  916.8 15.9 %psum.7 = f32[6144]{0:T(1024)S(1)} all-reduce(f32[6144]{0:T(1024)S(1)} %pad_maximum_fusion.14), channel_id=1, replica_groups=mesh['section'=2,'row'=4,'col'=4] {'col'}, use_global_device_ids=true, to_apply=%region_32.33 | all-reduce | flops 6144 | bytes 49152 | tf_op jit(solution)/shard_map/psum | solution.py:631
  955.4 67.8 %collective-permute-done.23 = bf16[512,512]{1,0:T(8,128)(2,1)S(1)} collective-permute-done((bf16[512,512]{1,0:T(8,128)(2,1)S(1)}, bf16[512,512]{1,0:T(8,128)(2,1)S(1)}, u32[]{:S(2)}, u32[]{:S(2)}) %collective-permute-start.23) | collective-permute-done | bytes 524320 | tf_op jit(solution)/shard_map/ppermute | solution.py:525
  1023.4 38.1 %collective-permute-done.22 = bf16[512,512]{1,0:T(8,128)(2,1)S(1)} collective-permute-done((bf16[512,512]{1,0:T(8,128)(2,1)}, bf16[512,512]{1,0:T(8,128)(2,1)S(1)}, u32[]{:S(2)}, u32[]{:S(2)}) %collective-permute-start.22) | collective-permute-done | bytes 524320 | tf_op jit(solution)/shard_map/ppermute | solution.py:525
  1082.0 6.3 collective-permute-done.25
  1103.0 7.9 collective-permute-done.21
  1120.3 6.7 collective-permute-done.14
  (594 shorter events, 367.0 us)
Async XLA Ops:
  7.2 293.7 %all-gather.19.cloned.1.call-start = ((), (), s32[]{:S(2)}) async-start(), calls=%async_computation.11 | async-start | bytes 1310720 | tf_op jit(solution)/shard_map/all_gather | solution.py:585
  8.6 35.3 %collective-permute-start.11 = (bf16[1024,512]{1,0:T(8,128)(2,1)S(1)}, bf16[1024,512]{1,0:T(8,128)(2,1)S(1)}, u32[]{:S(2)}, u32[]{:S(2)}) collective-permute-start(bf16[1024,512]{1,0:T(8,128)(2,1)S(1)} %dynamic-slice_bitcast_fusion), channel_id=1, source_target_pairs={{16,0},{17,1},{18,2},{19,3},{20,4},{21,5},{22,6},{23,7},{24,8},{25... | collective-permute-start | bytes 3145736 | tf_op jit(solution)/shard_map/ppermute | solution.py:82
  43.8 261.0 %all-gather.23.cloned.1.call-start = ((), (), s32[]{:S(2)}) async-start(), calls=%async_computation.21 | async-start | bytes 3145728 | tf_op jit(solution)/shard_map/all_gather | solution.py:511
  45.8 42.4 %collective-permute-start.6 = (bf16[512,512]{1,0:T(8,128)(2,1)S(1)}, bf16[512,512]{1,0:T(8,128)(2,1)S(1)}, u32[]{:S(2)}, u32[]{:S(2)}) collective-permute-start(bf16[512,512]{1,0:T(8,128)(2,1)S(1)} %constant_dynamic-slice_fusion.4), channel_id=1, source_target_pairs={{0,2},{1,3},{2,0},{3,1},{4,6},{5,7},{6,4},{7,5},{8,10},{9,11},{10,... | collective-permute-start | bytes 1572872 | tf_op jit(solution)/shard_map/ppermute | solution.py:509
  50.3 39.3 %collective-permute-start.9 = (bf16[512,1024]{1,0:T(8,128)(2,1)}, bf16[512,1024]{1,0:T(8,128)(2,1)}, u32[]{:S(2)}, u32[]{:S(2)}) collective-permute-start(bf16[512,1024]{1,0:T(8,128)(2,1)} %dynamic-slice_bitcast_fusion.1), channel_id=1, source_target_pairs={{16,0},{17,1},{18,2},{19,3},{20,4},{21,5},{22,6},{23,7},{24,8},{25... | collective-permute-start | bytes 3145736 | tf_op jit(solution)/shard_map/ppermute | solution.py:82
  51.6 38.0 %collective-permute-start.3 = (bf16[512,1024]{1,0:T(8,128)(2,1)}, bf16[512,1024]{1,0:T(8,128)(2,1)}, u32[]{:S(2)}, u32[]{:S(2)}) collective-permute-start(bf16[512,1024]{1,0:T(8,128)(2,1)} %dynamic-slice_bitcast_fusion.1), channel_id=1, source_target_pairs={{0,16},{1,17},{2,18},{3,19},{4,20},{5,21},{6,22},{7,23},{8,24},{9,... | collective-permute-start | bytes 3145736 | tf_op jit(solution)/shard_map/ppermute | solution.py:82
  89.6 218.1 %all-gather.21.cloned.1.call-start = ((), (), s32[]{:S(2)}) async-start(), calls=%async_computation.20 | async-start | bytes 3145728 | tf_op jit(solution)/shard_map/all_gather | solution.py:511
  92.5 34.5 %collective-permute-start.4 = (bf16[512,512]{1,0:T(8,128)(2,1)S(1)}, bf16[512,512]{1,0:T(8,128)(2,1)S(1)}, u32[]{:S(2)}, u32[]{:S(2)}) collective-permute-start(bf16[512,512]{1,0:T(8,128)(2,1)S(1)} %constant_dynamic-slice_fusion.5), channel_id=1, source_target_pairs={{0,2},{1,3},{2,0},{3,1},{4,6},{5,7},{6,4},{7,5},{8,10},{9,11},{10,... | collective-permute-start | bytes 1572872 | tf_op jit(solution)/shard_map/ppermute | solution.py:509
  92.6 47.4 %collective-permute-start.10 = (bf16[512,512]{1,0:T(8,128)(2,1)S(1)}, bf16[512,512]{1,0:T(8,128)(2,1)S(1)}, u32[]{:S(2)}, u32[]{:S(2)}) collective-permute-start(bf16[512,512]{1,0:T(8,128)(2,1)S(1)} %constant_dynamic-slice_fusion.3), channel_id=1, source_target_pairs={{0,2},{1,3},{2,0},{3,1},{4,6},{5,7},{6,4},{7,5},{8,10},{9,11},{10,... | collective-permute-start | bytes 1572872 | tf_op jit(solution)/shard_map/ppermute | solution.py:509
  141.6 179.5 %all-gather.27.cloned.1.call-start = ((), (), s32[]{:S(2)}) async-start(), calls=%async_computation.23 | async-start | bytes 3145728 | tf_op jit(solution)/shard_map/all_gather | solution.py:511
  167.2 156.7 %all-gather.25.cloned.1.call-start = ((), (), s32[]{:S(2)}) async-start(), calls=%async_computation.22 | async-start | bytes 3145728 | tf_op jit(solution)/shard_map/all_gather | solution.py:511
  168.4 175.6 %all-gather.13.cloned.1.call-start = ((), (), s32[]{:S(2)}) async-start(), calls=%async_computation.8 | async-start | bytes 3932160 | tf_op jit(solution)/shard_map/all_gather | solution.py:583
  193.8 178.4 %all-gather.15.cloned.1.call-start = ((), (), s32[]{:S(2)}) async-start(), calls=%async_computation.9 | async-start | bytes 1310720 | tf_op jit(solution)/shard_map/all_gather | solution.py:585
  194.1 88.1 %collective-permute-start = (f32[12288]{0:T(1024)S(1)}, f32[12288]{0:T(1024)S(1)}, u32[]{:S(2)}, u32[]{:S(2)}) collective-permute-start(f32[12288]{0:T(1024)S(1)} %constant_dynamic-update-slice_fusion.5), channel_id=1, source_target_pairs={{0,16},{16,0},{1,17},{17,1},{2,18},{18,2},{3,19},{19,3},{4,20},{20... | collective-permute-start | bytes 147464 | tf_op jit(solution)/shard_map/ppermute | solution.py:564
  282.2 221.1 %all-gather.17.cloned.1.call-start = ((), (), s32[]{:S(2)}) async-start(), calls=%async_computation.10 | async-start | bytes 3932160 | tf_op jit(solution)/shard_map/all_gather | solution.py:583
  290.4 649.9 %reduce-scatter.15.cloned.1.call-start = ((), (), s32[]{:S(2)}) async-start(), calls=%async_computation.15 | async-start | bytes 1310720 | tf_op jit(solution)/shard_map/reduce_scatter | solution.py:534
  553.5 390.4 %reduce-scatter.13.cloned.1.call-start = ((), (), s32[]{:S(2)}) async-start(), calls=%async_computation.14 | async-start | bytes 1310720 | tf_op jit(solution)/shard_map/reduce_scatter | solution.py:534
  672.9 272.4 %reduce-scatter.23.cloned.1.call-start = ((), (), s32[]{:S(2)}) async-start(), calls=%async_computation.19 | async-start | bytes 3145728 | tf_op jit(solution)/shard_map/reduce_scatter | solution.py:523
  683.9 263.2 %reduce-scatter.19.cloned.1.call-start = ((), (), s32[]{:S(2)}) async-start(), calls=%async_computation.17 | async-start | bytes 3145728 | tf_op jit(solution)/shard_map/reduce_scatter | solution.py:523
  691.7 259.8 %reduce-scatter.21.cloned.1.call-start = ((), (), s32[]{:S(2)}) async-start(), calls=%async_computation.18 | async-start | bytes 3145728 | tf_op jit(solution)/shard_map/reduce_scatter | solution.py:523
  703.9 250.2 %reduce-scatter.17.cloned.1.call-start = ((), (), s32[]{:S(2)}) async-start(), calls=%async_computation.16 | async-start | bytes 3145728 | tf_op jit(solution)/shard_map/reduce_scatter | solution.py:523
  719.9 375.3 %reduce-scatter.11.cloned.1.call-start = ((), (), s32[]{:S(2)}) async-start(), calls=%async_computation.13 | async-start | bytes 3932160 | tf_op jit(solution)/shard_map/reduce_scatter | solution.py:532
  726.7 370.9 %reduce-scatter.9.cloned.1.call-start = ((), (), s32[]{:S(2)}) async-start(), calls=%async_computation.12 | async-start | bytes 3932160 | tf_op jit(solution)/shard_map/reduce_scatter | solution.py:532
  746.1 170.6 %collective-permute-start.15 = (f32[1792]{0:T(1024)S(1)}, f32[1792]{0:T(1024)S(1)}, u32[]{:S(2)}, u32[]{:S(2)}) collective-permute-start(f32[1792]{0:T(1024)S(1)} %get-tuple-element.127), channel_id=1, source_target_pairs={{0,16},{16,0},{1,17},{17,1},{2,18},{18,2},{3,19},{19,3},{4,20},{20... | collective-permute-start | bytes 21512 | tf_op jit(solution)/shard_map/ppermute | solution.py:630
  940.3 138.2 %collective-permute-start.17 = (bf16[256,512]{1,0:T(8,128)(2,1)}, bf16[256,512]{1,0:T(8,128)(2,1)S(1)}, u32[]{:S(2)}, u32[]{:S(2)}) collective-permute-start(bf16[256,512]{1,0:T(8,128)(2,1)} %reduce-scatter.15.cloned.1.call-done), channel_id=1, source_target_pairs={{0,16},{1,17},{2,18},{3,19},{4,20},{5,21},{6,22},{7,23},{8,24},{9,... | collective-permute-start | bytes 786440 | tf_op jit(solution)/shard_map/ppermute | solution.py:608
  943.9 135.9 %collective-permute-start.16 = (bf16[256,512]{1,0:T(8,128)(2,1)}, bf16[256,512]{1,0:T(8,128)(2,1)}, u32[]{:S(2)}, u32[]{:S(2)}) collective-permute-start(bf16[256,512]{1,0:T(8,128)(2,1)} %reduce-scatter.13.cloned.1.call-done), channel_id=1, source_target_pairs={{16,0},{17,1},{18,2},{19,3},{20,4},{21,5},{22,6},{23,7},{24,8},{25... | collective-permute-start | bytes 786440 | tf_op jit(solution)/shard_map/ppermute | solution.py:608
  946.5 76.6 %collective-permute-start.23 = (bf16[512,512]{1,0:T(8,128)(2,1)S(1)}, bf16[512,512]{1,0:T(8,128)(2,1)S(1)}, u32[]{:S(2)}, u32[]{:S(2)}) collective-permute-start(bf16[512,512]{1,0:T(8,128)(2,1)S(1)} %select_bitcast_fusion), channel_id=1, source_target_pairs={{0,2},{1,3},{2,0},{3,1},{4,6},{5,7},{6,4},{7,5},{8,10},{9,11},{10,... | collective-permute-start | bytes 1572872 | tf_op jit(solution)/shard_map/ppermute | solution.py:525
  949.1 116.0 %collective-permute-start.19 = (bf16[512,512]{1,0:T(8,128)(2,1)}, bf16[512,512]{1,0:T(8,128)(2,1)S(1)}, u32[]{:S(2)}, u32[]{:S(2)}) collective-permute-start(bf16[512,512]{1,0:T(8,128)(2,1)} %select_bitcast_fusion.2), channel_id=1, source_target_pairs={{0,2},{1,3},{2,0},{3,1},{4,6},{5,7},{6,4},{7,5},{8,10},{9,11},{10,... | collective-permute-start | bytes 1572872 | tf_op jit(solution)/shard_map/ppermute | solution.py:525
  953.6 107.8 %collective-permute-start.22 = (bf16[512,512]{1,0:T(8,128)(2,1)}, bf16[512,512]{1,0:T(8,128)(2,1)S(1)}, u32[]{:S(2)}, u32[]{:S(2)}) collective-permute-start(bf16[512,512]{1,0:T(8,128)(2,1)} %select_bitcast_fusion.1), channel_id=1, source_target_pairs={{0,2},{1,3},{2,0},{3,1},{4,6},{5,7},{6,4},{7,5},{8,10},{9,11},{10,... | collective-permute-start | bytes 1572872 | tf_op jit(solution)/shard_map/ppermute | solution.py:525
  1023.2 49.5 %collective-permute-start.18 = (bf16[512,512]{1,0:T(8,128)(2,1)S(1)}, bf16[512,512]{1,0:T(8,128)(2,1)S(1)}, u32[]{:S(2)}, u32[]{:S(2)}) collective-permute-start(bf16[512,512]{1,0:T(8,128)(2,1)S(1)} %select_bitcast_fusion.3), channel_id=1, source_target_pairs={{0,2},{1,3},{2,0},{3,1},{4,6},{5,7},{6,4},{7,5},{8,10},{9,11},{10,... | collective-permute-start | bytes 1572872 | tf_op jit(solution)/shard_map/ppermute | solution.py:525
  1072.7 38.2 %collective-permute-start.21 = (bf16[512,1024]{1,0:T(8,128)(2,1)}, bf16[512,1024]{1,0:T(8,128)(2,1)}, u32[]{:S(2)}, u32[]{:S(2)}) collective-permute-start(bf16[512,1024]{1,0:T(8,128)(2,1)} %pad_maximum_fusion.7), channel_id=1, source_target_pairs={{0,16},{1,17},{2,18},{3,19},{4,20},{5,21},{6,22},{7,23},{8,24},{9,... | collective-permute-start | bytes 3145736 | tf_op jit(solution)/shard_map/ppermute | solution.py:608
  1078.5 37.2 %collective-permute-start.20 = (bf16[512,1024]{1,0:T(8,128)(2,1)}, bf16[512,1024]{1,0:T(8,128)(2,1)}, u32[]{:S(2)}, u32[]{:S(2)}) collective-permute-start(bf16[512,1024]{1,0:T(8,128)(2,1)} %pad_maximum_fusion.6), channel_id=1, source_target_pairs={{16,0},{17,1},{18,2},{19,3},{20,4},{21,5},{22,6},{23,7},{24,8},{25... | collective-permute-start | bytes 3145736 | tf_op jit(solution)/shard_map/ppermute | solution.py:608
  (143 other events, 2214.9 us)
Sparse Core Ops, SparseCore 0:
  44.0 42.9 all-gather.18
  89.7 56.5 all-gather.22
  148.4 40.1 all-gather.20
  190.5 44.2 all-gather.26
  236.2 43.4 all-gather.24
  281.1 62.8 all-gather.12
  345.6 26.6 all-gather.14
  373.8 99.3 all-gather.16
  553.7 24.9 reduce-scatter.14
  673.0 24.6 reduce-scatter.12
  700.0 30.4 reduce-scatter.22
  732.5 31.8 reduce-scatter.18
  766.7 43.1 reduce-scatter.20
  812.0 31.8 reduce-scatter.16
  846.1 72.5 reduce-scatter.10
  921.4 99.3 reduce-scatter.8
